TPU v7x, 768 devices: a whole 4x8x12 slice. The times are simulated.
768 devices in a mesh: rep: 4 (over y_lo, core), row: 16 (over y_hi, x), col: 12 (over z).
Axes of the slice: x: 4, y: 8 (y_hi: 4, y_lo: 2; y = y_hi * 2 + y_lo), z: 12, core: 2. Of those that a mesh axis runs over, the one named last changes fastest.
Arguments:
- delta: bfloat16 [4, 8192, 4608], P('rep', 'row', 'col'), may hold values from -6 to 6
- params: float32 [8192, 4608], P('row', 'col'), may hold values from -6 to 6
- momentum: float32 [8192, 4608], P('row', 'col'), may hold values from -3 to 3
Outputs:
- params_next: float32 [8192, 4608], P('row', 'col')
- momentum_next: float32 [8192, 4608], P('row', 'col')
- weights: bfloat16 [8192, 4608], P(None, 'col')
All inputs are finite; a program needn't handle non-finite values.
Results may differ from a plain program's by a relative error of at most 0.0075.
Values may be sent and summed in bfloat16 or wider, within the bound.
No kernel may reach another device: no remote copies, remote signals or barrier semaphores. Data moves between devices by JAX's collectives and lax.ppermute only.
A program may use at most 64 MiB of HBM per device.

v0:
```python
import jax
import jax.numpy as jnp
from jax import lax
from jax.experimental import pallas as pl
from jax.experimental.pallas import tpu as pltpu
from jax.sharding import PartitionSpec as P


PLANE = ("rep", "row")
NX, NY = 4, 8


def index(x, y, core):
    return ((y % NY % 2) * 2 + core) * (NX * NY // 2) + (y % NY // 2) * NX + x % NX


def beside(i, core):
    return i + 1 - 2 * ((i + core) % 2)


def send(array, partner):
    pairs = [
        (index(x, y, core), index(*partner(x, y, core)))
        for x in range(NX)
        for y in range(NY)
        for core in range(2)
    ]
    return lax.ppermute(array, PLANE, pairs)


def far_groups():
    return [
        [index(x + 2 * j, y + 2 * i, core) for i in range(NY // 2) for j in range(NX // 2)]
        for x in range(2)
        for y in range(2)
        for core in range(2)
    ]


def update(average, params, momentum):
    momentum_next = 0.9 * momentum + average
    params_next = params - 0.7 * (average + 0.9 * momentum_next)
    return (params_next, momentum_next)


def quarter_kernel(parts_ref, params_ref, momentum_ref, average_ref, weights_ref):
    reps = parts_ref.shape[0]
    total = parts_ref[0].astype(jnp.float32)
    for i in range(1, reps):
        total += parts_ref[i].astype(jnp.float32)
    average = total / reps
    average_ref[...] = average
    params_next, _ = update(average, params_ref[...], momentum_ref[...])
    for i in range(weights_ref.shape[0]):
        weights_ref[i] = params_next.astype(jnp.bfloat16)


def whole_kernel(own_ref, y_ref, core_ref, both_ref, params_ref, momentum_ref, params_out, momentum_out):
    rep = lax.axis_index("rep")
    y, core = rep // 2, lax.rem(rep, 2)
    rows = own_ref.shape[0]
    for ref, flip_y, flip_core in ((own_ref, 0, 0), (y_ref, 1, 0), (core_ref, 0, 1), (both_ref, 1, 1)):
        block = (1 - y if flip_y else y) * 2 + (1 - core if flip_core else core)
        at = pl.ds(pl.multiple_of(block * rows, rows), rows)
        params_out[at], momentum_out[at] = update(ref[...], params_ref[at], momentum_ref[at])


def place_kernel(flips, n, *refs):
    out_ref, sems = refs[-2:]
    rep, row = lax.axis_index("rep"), lax.axis_index("row")
    x, y, core = lax.rem(row, 2), rep // 2, lax.rem(rep, 2)
    copies = []
    for i, (ref, (fx, fy, fc)) in enumerate(zip(refs[:n], flips)):
        far, rows, _ = ref.shape
        near = ((1 - x if fx else x) * 2 + (1 - y if fy else y)) * 2 + (1 - core if fc else core)
        for k in range(far):
            at = pl.multiple_of((k * 8 + near) * rows, rows)
            copy = pltpu.make_async_copy(ref.at[k], out_ref.at[pl.ds(at, rows)], sems.at[i, k])
            copy.start()
            copies.append(copy)
    for copy in copies:
        copy.wait()


def place(blocks, out, shape):
    arrays, flips = zip(*blocks)
    n = len(arrays)
    far = arrays[0].shape[0]
    kernel = lambda *refs: place_kernel(flips, n, *refs)
    operands = arrays if out is None else (*arrays, out)
    return pl.pallas_call(
        kernel,
        name="place",
        out_shape=jax.ShapeDtypeStruct(shape, jnp.bfloat16),
        in_specs=[pl.BlockSpec(memory_space=pl.ANY)] * len(operands),
        out_specs=pl.BlockSpec(memory_space=pl.ANY),
        scratch_shapes=[pltpu.SemaphoreType.DMA((n, far))],
        input_output_aliases={} if out is None else {n: 0},
        compiler_params=pltpu.CompilerParams(vmem_limit_bytes=1 << 20),
        cost_estimate=pl.CostEstimate(
            flops=n * 1000000, bytes_accessed=2 * 2 * n * arrays[0].size, transcendentals=0
        ),
    )(*operands)


VMEM = pl.BlockSpec(memory_space=pltpu.VMEM)


def on_device(delta, params, momentum):
    reps = lax.axis_size("rep")
    rows, columns = params.shape[0] // reps, params.shape[1]
    groups = far_groups()
    block = jax.ShapeDtypeStruct((rows, columns), jnp.float32)
    whole = jax.ShapeDtypeStruct(params.shape, jnp.float32)
    small = pltpu.CompilerParams(vmem_limit_bytes=8 << 20)

    parts = lax.all_to_all(delta[0].reshape(reps, rows, columns), "rep", 0, 0, tiled=True)
    first_row = lax.axis_index("rep") * rows
    average, weights = pl.pallas_call(
        quarter_kernel,
        name="quarter",
        out_shape=(block, jax.ShapeDtypeStruct((len(groups[0]), rows, columns), jnp.bfloat16)),
        in_specs=[VMEM] * 3,
        out_specs=(VMEM, VMEM),
        compiler_params=small,
    )(
        parts,
        lax.dynamic_slice_in_dim(params, first_row, rows, 0),
        lax.dynamic_slice_in_dim(momentum, first_row, rows, 0),
    )

    own = lax.all_to_all(weights, PLANE, 0, 0, axis_index_groups=groups, tiled=True)
    by_x = send(own, lambda x, y, core: (beside(x, core), y, core))
    by_y = send(own, lambda x, y, core: (x, beside(y, core), core))
    by_both = send(own, lambda x, y, core: (beside(x, core), beside(y, core), core))
    average_y = send(average, lambda x, y, core: (x, y ^ 1, core))
    swap = lambda array: send(array, lambda x, y, core: (x, y, 1 - core))
    own_swap = swap(own)
    average_swap = swap(average)
    x_swap = swap(by_x)
    y_swap = swap(by_y)
    average_y_swap = swap(average_y)
    both_swap = swap(by_both)

    shape = (params.shape[0] * NX * NY // 2, columns)
    out = place(
        [(own, (0, 0, 0)), (own_swap, (0, 0, 1)), (by_x, (1, 0, 0)), (by_y, (0, 1, 0))],
        None,
        shape,
    )
    out = place(
        [(x_swap, (1, 0, 1)), (y_swap, (0, 1, 1)), (by_both, (1, 1, 0)), (both_swap, (1, 1, 1))],
        out,
        shape,
    )

    params_next, momentum_next = pl.pallas_call(
        whole_kernel,
        name="whole",
        out_shape=(whole, whole),
        in_specs=[VMEM] * 6,
        out_specs=(VMEM, VMEM),
        compiler_params=small,
        cost_estimate=pl.CostEstimate(flops=1000000, bytes_accessed=5 << 20, transcendentals=0),
    )(average, average_y, average_swap, average_y_swap, params, momentum)
    return (params_next, momentum_next, out)


def solution(mesh):
    return jax.shard_map(
        on_device,
        mesh=mesh,
        in_specs=(P("rep", "row", "col"), P("row", "col"), P("row", "col")),
        out_specs=(P("row", "col"), P("row", "col"), P(None, "col")),
        check_vma=False,
    )
```

profile of v0, /device:TPU:1, one launch (start us, length us, event | category | flops | bytes accessed | tf_op | source)
XLA Modules:
  0.0 98.0 jit_solution(5212060441839870457)
XLA Ops:
  0.6 13.9 %all-to-all-start = ((bf16[4,128,384]{2,1,0:T(8,128)(2,1)}), bf16[4,128,384]{2,1,0:T(8,128)(2,1)S(1)}, u32[]{:S(2)}, u32[]{:S(2)}) async-start(bf16[4,128,384]{2,1,0:T(8,128)(2,1)} %bitcast.1), calls=%async_computation | async-start | bytes 786432 | tf_op jit(solution)/shard_map/all_to_all | solution.py:117
  14.5 1.0 %constant_dynamic-slice_fusion = (f32[128,384]{1,0:T(8,128)S(1)}, f32[128,384]{1,0:T(8,128)S(1)}) fusion(f32[512,384]{1,0:T(8,128)} %momentum_ref.1, s32[]{:T(128)S(6)} %select_n.4, f32[512,384]{1,0:T(8,128)} %params_ref.1), kind=kLoop, calls=%fused_computation | loop fusion | bytes 786436 | tf_op jit(solution)/shard_map/dynamic_slice | solution.py:129
  15.6 5.4 %all-to-all-done.parts_ref = bf16[4,128,384]{2,1,0:T(8,128)(2,1)S(1)} async-done(((bf16[4,128,384]{2,1,0:T(8,128)(2,1)}), bf16[4,128,384]{2,1,0:T(8,128)(2,1)S(1)}, u32[]{:S(2)}, u32[]{:S(2)}) %all-to-all-start) | async-done | bytes 393248 | tf_op jit(solution)/shard_map/all_to_all | solution.py:117
  21.1 24.8 %all_to_all.10.refs_0_ = bf16[8,128,384]{2,1,0:T(8,128)(2,1)S(1)} all-to-all(bf16[8,128,384]{2,1,0:T(8,128)(2,1)S(1)} %get-tuple-element.10), channel_id=1, replica_groups={{0,24,48,72,96,120,144,168},{192,216,240,264,288,312,336,360},{384,408,..., dimensions={0} | all-to-all | bytes 1572864 | tf_op jit(solution)/shard_map/all_to_all | solution.py:132
  45.9 1.9 %collective-permute-start.3 = (bf16[8,128,384]{2,1,0:T(8,128)(2,1)S(1)}, bf16[8,128,384]{2,1,0:T(8,128)(2,1)S(1)}, u32[]{:S(2)}, u32[]{:S(2)}) collective-permute-start(bf16[8,128,384]{2,1,0:T(8,128)(2,1)S(1)} %all_to_all.10.refs_0_), channel_id=1, source_target_pairs={{0,12},{192,228},{384,396},{576,612},{48,60},{240,276},{432,444},{... | collective-permute-start | bytes 2359304 | tf_op jit(solution)/shard_map/ppermute | solution.py:28
  47.9 1.9 %collective-permute-start.5 = (bf16[8,128,384]{2,1,0:T(8,128)(2,1)S(1)}, bf16[8,128,384]{2,1,0:T(8,128)(2,1)S(1)}, u32[]{:S(2)}, u32[]{:S(2)}) collective-permute-start(bf16[8,128,384]{2,1,0:T(8,128)(2,1)S(1)} %all_to_all.10.refs_0_), channel_id=1, source_target_pairs={{0,384},{192,720},{384,0},{576,240},{48,432},{240,576},{432,48},{6... | collective-permute-start | bytes 2359304 | tf_op jit(solution)/shard_map/ppermute | solution.py:28
  49.8 7.0 %collective-permute-start.7 = (bf16[8,128,384]{2,1,0:T(8,128)(2,1)S(1)}, bf16[8,128,384]{2,1,0:T(8,128)(2,1)S(1)}, u32[]{:S(2)}, u32[]{:S(2)}) collective-permute-start(bf16[8,128,384]{2,1,0:T(8,128)(2,1)S(1)} %all_to_all.10.refs_0_), channel_id=1, source_target_pairs={{0,396},{192,756},{384,12},{576,276},{48,444},{240,612},{432,60},{... | collective-permute-start | bytes 2359304 | tf_op jit(solution)/shard_map/ppermute | solution.py:28
  56.7 1.9 %collective-permute-start.9 = (bf16[8,128,384]{2,1,0:T(8,128)(2,1)S(1)}, bf16[8,128,384]{2,1,0:T(8,128)(2,1)S(1)}, u32[]{:S(2)}, u32[]{:S(2)}) collective-permute-start(bf16[8,128,384]{2,1,0:T(8,128)(2,1)S(1)} %all_to_all.10.refs_0_), channel_id=1, source_target_pairs={{0,192},{192,0},{384,576},{576,384},{48,240},{240,48},{432,624},{6... | collective-permute-start | bytes 2359304 | tf_op jit(solution)/shard_map/ppermute | solution.py:28
  58.7 1.2 %collective-permute-done.3.refs_2_ = bf16[8,128,384]{2,1,0:T(8,128)(2,1)S(1)} collective-permute-done((bf16[8,128,384]{2,1,0:T(8,128)(2,1)S(1)}, bf16[8,128,384]{2,1,0:T(8,128)(2,1)S(1)}, u32[]{:S(2)}, u32[]{:S(2)}) %collective-permute-start.3) | collective-permute-done | bytes 786464 | tf_op jit(solution)/shard_map/ppermute | solution.py:28
  59.9 3.3 %collective-permute-start.4 = (bf16[8,128,384]{2,1,0:T(8,128)(2,1)S(1)}, bf16[8,128,384]{2,1,0:T(8,128)(2,1)S(1)}, u32[]{:S(2)}, u32[]{:S(2)}) collective-permute-start(bf16[8,128,384]{2,1,0:T(8,128)(2,1)S(1)} %collective-permute-done.3.refs_2_), channel_id=1, source_target_pairs={{0,192},{192,0},{384,576},{576,384},{48,240},{240,48},{432,624},{6... | collective-permute-start | bytes 2359304 | tf_op jit(solution)/shard_map/ppermute | solution.py:28
  63.2 1.9 %collective-permute-start.6 = (bf16[8,128,384]{2,1,0:T(8,128)(2,1)S(1)}, bf16[8,128,384]{2,1,0:T(8,128)(2,1)S(1)}, u32[]{:S(2)}, u32[]{:S(2)}) collective-permute-start(bf16[8,128,384]{2,1,0:T(8,128)(2,1)S(1)} %collective-permute-done.5.refs_3_), channel_id=1, source_target_pairs={{0,192},{192,0},{384,576},{576,384},{48,240},{240,48},{432,624},{6... | collective-permute-start | bytes 2359304 | tf_op jit(solution)/shard_map/ppermute | solution.py:28
  65.2 7.5 %collective-permute-done.7.refs_2_ = bf16[8,128,384]{2,1,0:T(8,128)(2,1)S(1)} collective-permute-done((bf16[8,128,384]{2,1,0:T(8,128)(2,1)S(1)}, bf16[8,128,384]{2,1,0:T(8,128)(2,1)S(1)}, u32[]{:S(2)}, u32[]{:S(2)}) %collective-permute-start.7) | collective-permute-done | bytes 786464 | tf_op jit(solution)/shard_map/ppermute | solution.py:28
  72.6 2.4 %collective-permute-start.8 = (bf16[8,128,384]{2,1,0:T(8,128)(2,1)S(1)}, bf16[8,128,384]{2,1,0:T(8,128)(2,1)S(1)}, u32[]{:S(2)}, u32[]{:S(2)}) collective-permute-start(bf16[8,128,384]{2,1,0:T(8,128)(2,1)S(1)} %collective-permute-done.7.refs_2_), channel_id=1, source_target_pairs={{0,192},{192,0},{384,576},{576,384},{48,240},{240,48},{432,624},{6... | collective-permute-start | bytes 2359304 | tf_op jit(solution)/shard_map/ppermute | solution.py:28
  75.0 2.7 %collective-permute-start = (f32[128,384]{1,0:T(8,128)S(1)}, f32[128,384]{1,0:T(8,128)S(1)}, u32[]{:S(2)}, u32[]{:S(2)}) collective-permute-start(f32[128,384]{1,0:T(8,128)S(1)} %get-tuple-element.7.own_ref), channel_id=1, source_target_pairs={{0,384},{192,576},{384,0},{576,192},{48,432},{240,624},{432,48},{6... | collective-permute-start | bytes 589832 | tf_op jit(solution)/shard_map/ppermute | solution.py:28
  77.7 5.7 %collective-permute-done.y_ref = f32[128,384]{1,0:T(8,128)S(1)} collective-permute-done((f32[128,384]{1,0:T(8,128)S(1)}, f32[128,384]{1,0:T(8,128)S(1)}, u32[]{:S(2)}, u32[]{:S(2)}) %collective-permute-start) | collective-permute-done | bytes 196640 | tf_op jit(solution)/shard_map/ppermute | solution.py:28
  83.4 2.8 %collective-permute-start.1 = (f32[128,384]{1,0:T(8,128)S(1)}, f32[128,384]{1,0:T(8,128)S(1)}, u32[]{:S(2)}, u32[]{:S(2)}) collective-permute-start(f32[128,384]{1,0:T(8,128)S(1)} %get-tuple-element.7.own_ref), channel_id=1, source_target_pairs={{0,192},{192,0},{384,576},{576,384},{48,240},{240,48},{432,624},{6... | collective-permute-start | bytes 589832 | tf_op jit(solution)/shard_map/ppermute | solution.py:28
  86.1 1.0 %collective-permute-done.1.core_ref = f32[128,384]{1,0:T(8,128)S(1)} collective-permute-done((f32[128,384]{1,0:T(8,128)S(1)}, f32[128,384]{1,0:T(8,128)S(1)}, u32[]{:S(2)}, u32[]{:S(2)}) %collective-permute-start.1) | collective-permute-done | bytes 196640 | tf_op jit(solution)/shard_map/ppermute | solution.py:28
  87.2 2.3 %collective-permute-start.2 = (f32[128,384]{1,0:T(8,128)S(1)}, f32[128,384]{1,0:T(8,128)S(1)}, u32[]{:S(2)}, u32[]{:S(2)}) collective-permute-start(f32[128,384]{1,0:T(8,128)S(1)} %collective-permute-done.y_ref), channel_id=1, source_target_pairs={{0,192},{192,0},{384,576},{576,384},{48,240},{240,48},{432,624},{6... | collective-permute-start | bytes 589832 | tf_op jit(solution)/shard_map/ppermute | solution.py:28
  89.5 1.0 %collective-permute-done.2.both_ref = f32[128,384]{1,0:T(8,128)S(1)} collective-permute-done((f32[128,384]{1,0:T(8,128)S(1)}, f32[128,384]{1,0:T(8,128)S(1)}, u32[]{:S(2)}, u32[]{:S(2)}) %collective-permute-start.2) | collective-permute-done | bytes 196640 | tf_op jit(solution)/shard_map/ppermute | solution.py:28
  90.5 1.1 %copy-done = f32[512,384]{1,0:T(8,128)S(1)} copy-done((f32[512,384]{1,0:T(8,128)S(1)}, f32[512,384]{1,0:T(8,128)}, u32[]{:S(2)}) %copy-start) | copy-done | bytes 786456
  91.6 1.1 %copy-done.1 = f32[512,384]{1,0:T(8,128)S(1)} copy-done((f32[512,384]{1,0:T(8,128)S(1)}, f32[512,384]{1,0:T(8,128)}, u32[]{:S(2)}) %copy-start.1) | copy-done | bytes 786456
  92.8 1.3 %whole.1 = (f32[512,384]{1,0:T(8,128)}, f32[512,384]{1,0:T(8,128)}) custom-call(f32[128,384]{1,0:T(8,128)S(1)} %get-tuple-element.7.own_ref, f32[128,384]{1,0:T(8,128)S(1)} %collective-permute-done.y_ref, f32[128,384]{1,0:T(8,128)S(1)} %collective-permute-done.1.core_ref, f32[128,384]{1,0:T(8,128)S(1)} %collective-permute-done.2.both_ref, ...), custom_call_target="tpu_custom_call" | custom-call | flops 1000000 | bytes 5242880 | tf_op jit(solution)/shard_map/whole/pallas_call | solution.py:157
  94.1 1.9 %place.2.refs_4_ = bf16[8192,384]{1,0:T(8,128)(2,1)} custom-call(bf16[8,128,384]{2,1,0:T(8,128)(2,1)S(1)} %all_to_all.10.refs_0_, bf16[8,128,384]{2,1,0:T(8,128)(2,1)S(1)} %collective-permute-done.9.refs_1_, bf16[8,128,384]{2,1,0:T(8,128)(2,1)S(1)} %collective-permute-done.3.refs_2_, bf16[8,128,384]{2,1,0:T(8,128)(2,1)S(1)} %collective-permute-done.5.refs_3_), custom_call_target="tpu_custom_call" | custom-call | flops 4000000 | bytes 6291456 | tf_op jit(solution)/shard_map/place/pallas_call | solution.py:91
  96.1 1.9 %place.3 = bf16[8192,384]{1,0:T(8,128)(2,1)} custom-call(bf16[8,128,384]{2,1,0:T(8,128)(2,1)S(1)} %collective-permute-done.4.refs_0_, bf16[8,128,384]{2,1,0:T(8,128)(2,1)S(1)} %collective-permute-done.6.refs_1_, bf16[8,128,384]{2,1,0:T(8,128)(2,1)S(1)} %collective-permute-done.7.refs_2_, ...), custom_call_target="tpu_custom_call", output_to_operand_aliasing={{}: (4, {})} | custom-call | flops 4000000 | bytes 6291456 | tf_op jit(solution)/shard_map/place/pallas_call | solution.py:91
  (8 shorter events, 0.1 us)
Async XLA Ops:
  0.6 20.4 %all-to-all-start = ((bf16[4,128,384]{2,1,0:T(8,128)(2,1)}), bf16[4,128,384]{2,1,0:T(8,128)(2,1)S(1)}, u32[]{:S(2)}, u32[]{:S(2)}) async-start(bf16[4,128,384]{2,1,0:T(8,128)(2,1)} %bitcast.1), calls=%async_computation | async-start | bytes 786432 | tf_op jit(solution)/shard_map/all_to_all | solution.py:117
  45.9 13.9 %collective-permute-start.3 = (bf16[8,128,384]{2,1,0:T(8,128)(2,1)S(1)}, bf16[8,128,384]{2,1,0:T(8,128)(2,1)S(1)}, u32[]{:S(2)}, u32[]{:S(2)}) collective-permute-start(bf16[8,128,384]{2,1,0:T(8,128)(2,1)S(1)} %all_to_all.10.refs_0_), channel_id=1, source_target_pairs={{0,12},{192,228},{384,396},{576,612},{48,60},{240,276},{432,444},{... | collective-permute-start | bytes 2359304 | tf_op jit(solution)/shard_map/ppermute | solution.py:28
  47.9 15.4 %collective-permute-start.5 = (bf16[8,128,384]{2,1,0:T(8,128)(2,1)S(1)}, bf16[8,128,384]{2,1,0:T(8,128)(2,1)S(1)}, u32[]{:S(2)}, u32[]{:S(2)}) collective-permute-start(bf16[8,128,384]{2,1,0:T(8,128)(2,1)S(1)} %all_to_all.10.refs_0_), channel_id=1, source_target_pairs={{0,384},{192,720},{384,0},{576,240},{48,432},{240,576},{432,48},{6... | collective-permute-start | bytes 2359304 | tf_op jit(solution)/shard_map/ppermute | solution.py:28
  49.8 22.8 %collective-permute-start.7 = (bf16[8,128,384]{2,1,0:T(8,128)(2,1)S(1)}, bf16[8,128,384]{2,1,0:T(8,128)(2,1)S(1)}, u32[]{:S(2)}, u32[]{:S(2)}) collective-permute-start(bf16[8,128,384]{2,1,0:T(8,128)(2,1)S(1)} %all_to_all.10.refs_0_), channel_id=1, source_target_pairs={{0,396},{192,756},{384,12},{576,276},{48,444},{240,612},{432,60},{... | collective-permute-start | bytes 2359304 | tf_op jit(solution)/shard_map/ppermute | solution.py:28
  56.7 37.4 %collective-permute-start.9 = (bf16[8,128,384]{2,1,0:T(8,128)(2,1)S(1)}, bf16[8,128,384]{2,1,0:T(8,128)(2,1)S(1)}, u32[]{:S(2)}, u32[]{:S(2)}) collective-permute-start(bf16[8,128,384]{2,1,0:T(8,128)(2,1)S(1)} %all_to_all.10.refs_0_), channel_id=1, source_target_pairs={{0,192},{192,0},{384,576},{576,384},{48,240},{240,48},{432,624},{6... | collective-permute-start | bytes 2359304 | tf_op jit(solution)/shard_map/ppermute | solution.py:28
  59.9 36.2 %collective-permute-start.4 = (bf16[8,128,384]{2,1,0:T(8,128)(2,1)S(1)}, bf16[8,128,384]{2,1,0:T(8,128)(2,1)S(1)}, u32[]{:S(2)}, u32[]{:S(2)}) collective-permute-start(bf16[8,128,384]{2,1,0:T(8,128)(2,1)S(1)} %collective-permute-done.3.refs_2_), channel_id=1, source_target_pairs={{0,192},{192,0},{384,576},{576,384},{48,240},{240,48},{432,624},{6... | collective-permute-start | bytes 2359304 | tf_op jit(solution)/shard_map/ppermute | solution.py:28
  63.2 32.8 %collective-permute-start.6 = (bf16[8,128,384]{2,1,0:T(8,128)(2,1)S(1)}, bf16[8,128,384]{2,1,0:T(8,128)(2,1)S(1)}, u32[]{:S(2)}, u32[]{:S(2)}) collective-permute-start(bf16[8,128,384]{2,1,0:T(8,128)(2,1)S(1)} %collective-permute-done.5.refs_3_), channel_id=1, source_target_pairs={{0,192},{192,0},{384,576},{576,384},{48,240},{240,48},{432,624},{6... | collective-permute-start | bytes 2359304 | tf_op jit(solution)/shard_map/ppermute | solution.py:28
  72.6 23.5 %collective-permute-start.8 = (bf16[8,128,384]{2,1,0:T(8,128)(2,1)S(1)}, bf16[8,128,384]{2,1,0:T(8,128)(2,1)S(1)}, u32[]{:S(2)}, u32[]{:S(2)}) collective-permute-start(bf16[8,128,384]{2,1,0:T(8,128)(2,1)S(1)} %collective-permute-done.7.refs_2_), channel_id=1, source_target_pairs={{0,192},{192,0},{384,576},{576,384},{48,240},{240,48},{432,624},{6... | collective-permute-start | bytes 2359304 | tf_op jit(solution)/shard_map/ppermute | solution.py:28
  75.0 8.3 %collective-permute-start = (f32[128,384]{1,0:T(8,128)S(1)}, f32[128,384]{1,0:T(8,128)S(1)}, u32[]{:S(2)}, u32[]{:S(2)}) collective-permute-start(f32[128,384]{1,0:T(8,128)S(1)} %get-tuple-element.7.own_ref), channel_id=1, source_target_pairs={{0,384},{192,576},{384,0},{576,192},{48,432},{240,624},{432,48},{6... | collective-permute-start | bytes 589832 | tf_op jit(solution)/shard_map/ppermute | solution.py:28
  83.4 3.8 %collective-permute-start.1 = (f32[128,384]{1,0:T(8,128)S(1)}, f32[128,384]{1,0:T(8,128)S(1)}, u32[]{:S(2)}, u32[]{:S(2)}) collective-permute-start(f32[128,384]{1,0:T(8,128)S(1)} %get-tuple-element.7.own_ref), channel_id=1, source_target_pairs={{0,192},{192,0},{384,576},{576,384},{48,240},{240,48},{432,624},{6... | collective-permute-start | bytes 589832 | tf_op jit(solution)/shard_map/ppermute | solution.py:28
  87.2 3.3 %collective-permute-start.2 = (f32[128,384]{1,0:T(8,128)S(1)}, f32[128,384]{1,0:T(8,128)S(1)}, u32[]{:S(2)}, u32[]{:S(2)}) collective-permute-start(f32[128,384]{1,0:T(8,128)S(1)} %collective-permute-done.y_ref), channel_id=1, source_target_pairs={{0,192},{192,0},{384,576},{576,384},{48,240},{240,48},{432,624},{6... | collective-permute-start | bytes 589832 | tf_op jit(solution)/shard_map/ppermute | solution.py:28
  90.5 1.1 %copy-start = (f32[512,384]{1,0:T(8,128)S(1)}, f32[512,384]{1,0:T(8,128)}, u32[]{:S(2)}) copy-start(f32[512,384]{1,0:T(8,128)} %momentum_ref.1) | copy-start | bytes 2359300
  91.6 1.1 %copy-start.1 = (f32[512,384]{1,0:T(8,128)S(1)}, f32[512,384]{1,0:T(8,128)}, u32[]{:S(2)}) copy-start(f32[512,384]{1,0:T(8,128)} %params_ref.1) | copy-start | bytes 2359300
where the time goes:
time: 98.6 us; the launch traced here: 98 us
  starting transfers between devices  42 us (43%)
  blocking collectives  24.8 us (25%)
  waiting for transfers between devices  21.8 us (22%)
  Pallas kernels  5.31 us (5%)
  local copies, waits for them, and re-layouts  3.31 us (3%)
    ppermute x10, starting transfers between devices, send(): return lax.ppermute(array, PLANE, pairs)  28.1 us
    all_to_all x1, blocking collectives, on_device(): lax.all_to_all(weights, PLANE, 0, 0, axis_index_groups=groups, tiled=True)  24.8 us
    ppermute x10, waiting for transfers between devices, send(): return lax.ppermute(array, PLANE, pairs)  16.4 us
    all_to_all x1, starting transfers between devices, on_device(): lax.all_to_all(delta[0].reshape(reps, rows, columns), 'rep', 0, 0, tiled=...  13.9 us
    all_to_all x1, waiting for transfers between devices, on_device(): lax.all_to_all(delta[0].reshape(reps, rows, columns), 'rep', 0, 0, tiled=...  5.39 us
    pallas_call x2, Pallas kernels, place(): pl.pallas_call(kernel, name='place', out_shape=jax.ShapeDtypeStruct(shape...  3.87 us
    unnamed x4, local copies, waits for them, and re-layouts  2.27 us
  transfers between devices with their start and end apart: 11, of which 6 were waited for; matrix products, arithmetic and copies ran while one was open for 1% of the time, Pallas kernels for 3%

commit v1 on v0

--- a/solution.py
+++ b/solution.py
@@ -144,15 +144,19 @@
 
     shape = (params.shape[0] * NX * NY // 2, columns)
     out = place(
-        [(own, (0, 0, 0)), (own_swap, (0, 0, 1)), (by_x, (1, 0, 0)), (by_y, (0, 1, 0))],
+        [
+            (own, (0, 0, 0)),
+            (own_swap, (0, 0, 1)),
+            (by_x, (1, 0, 0)),
+            (x_swap, (1, 0, 1)),
+            (by_y, (0, 1, 0)),
+            (y_swap, (0, 1, 1)),
+        ],
         None,
         shape,
     )
-    out = place(
-        [(x_swap, (1, 0, 1)), (y_swap, (0, 1, 1)), (by_both, (1, 1, 0)), (both_swap, (1, 1, 1))],
-        out,
-        shape,
-    )
+    out = place([(by_both, (1, 1, 0))], out, shape)
+    out = place([(both_swap, (1, 1, 1))], out, shape)
 
     params_next, momentum_next = pl.pallas_call(
         whole_kernel,

time: 98.6 us -> 99.2 us (level)
    pallas_call x2 -> x3, Pallas kernels: 3.87 us -> 4.52 us  [place(): pl.pallas_call(kernel, name='place', out_shape=jax.ShapeDtypeStruct(shape...]
  transfers between devices with their start and end apart: 11 -> 11, of which waited for: 6 -> 6; matrix products, arithmetic and copies ran while one was open for 1% -> 1% of each run, Pallas kernels for 3% -> 5%
where the time goes in v1:
time: 99.2 us; the launch traced here: 98.7 us
  starting transfers between devices  42 us (42%)
  blocking collectives  24.8 us (25%)
  waiting for transfers between devices  21.8 us (22%)
  Pallas kernels  5.96 us (6%)
  local copies, waits for them, and re-layouts  3.31 us (3%)
    ppermute x10, starting transfers between devices, send(): return lax.ppermute(array, PLANE, pairs)  28.1 us
    all_to_all x1, blocking collectives, on_device(): lax.all_to_all(weights, PLANE, 0, 0, axis_index_groups=groups, tiled=True)  24.8 us
    ppermute x10, waiting for transfers between devices, send(): return lax.ppermute(array, PLANE, pairs)  16.4 us
    all_to_all x1, starting transfers between devices, on_device(): lax.all_to_all(delta[0].reshape(reps, rows, columns), 'rep', 0, 0, tiled=...  13.9 us
    all_to_all x1, waiting for transfers between devices, on_device(): lax.all_to_all(delta[0].reshape(reps, rows, columns), 'rep', 0, 0, tiled=...  5.39 us
    pallas_call x3, Pallas kernels, place(): pl.pallas_call(kernel, name='place', out_shape=jax.ShapeDtypeStruct(shape...  4.52 us
    unnamed x4, local copies, waits for them, and re-layouts  2.27 us
  transfers between devices with their start and end apart: 11, of which 6 were waited for; matrix products, arithmetic and copies ran while one was open for 1% of the time, Pallas kernels for 5%

profile of v1, /device:TPU:1, one launch (start us, length us, event | category | flops | bytes accessed | tf_op | source)
XLA Modules:
  0.0 98.7 jit_solution(14874309765395903304)
XLA Ops:
  0.6 13.9 %all-to-all-start = ((bf16[4,128,384]{2,1,0:T(8,128)(2,1)}), bf16[4,128,384]{2,1,0:T(8,128)(2,1)S(1)}, u32[]{:S(2)}, u32[]{:S(2)}) async-start(bf16[4,128,384]{2,1,0:T(8,128)(2,1)} %bitcast.1), calls=%async_computation | async-start | bytes 786432 | tf_op jit(solution)/shard_map/all_to_all | solution.py:117
  14.5 1.0 %constant_dynamic-slice_fusion = (f32[128,384]{1,0:T(8,128)S(1)}, f32[128,384]{1,0:T(8,128)S(1)}) fusion(f32[512,384]{1,0:T(8,128)} %momentum_ref.1, s32[]{:T(128)S(6)} %select_n.4, f32[512,384]{1,0:T(8,128)} %params_ref.1), kind=kLoop, calls=%fused_computation | loop fusion | bytes 786436 | tf_op jit(solution)/shard_map/dynamic_slice | solution.py:129
  15.6 5.4 %all-to-all-done.parts_ref = bf16[4,128,384]{2,1,0:T(8,128)(2,1)S(1)} async-done(((bf16[4,128,384]{2,1,0:T(8,128)(2,1)}), bf16[4,128,384]{2,1,0:T(8,128)(2,1)S(1)}, u32[]{:S(2)}, u32[]{:S(2)}) %all-to-all-start) | async-done | bytes 393248 | tf_op jit(solution)/shard_map/all_to_all | solution.py:117
  21.1 24.8 %all_to_all.10.refs_0_ = bf16[8,128,384]{2,1,0:T(8,128)(2,1)S(1)} all-to-all(bf16[8,128,384]{2,1,0:T(8,128)(2,1)S(1)} %get-tuple-element.10), channel_id=1, replica_groups={{0,24,48,72,96,120,144,168},{192,216,240,264,288,312,336,360},{384,408,..., dimensions={0} | all-to-all | bytes 1572864 | tf_op jit(solution)/shard_map/all_to_all | solution.py:132
  45.9 1.9 %collective-permute-start.6 = (bf16[8,128,384]{2,1,0:T(8,128)(2,1)S(1)}, bf16[8,128,384]{2,1,0:T(8,128)(2,1)S(1)}, u32[]{:S(2)}, u32[]{:S(2)}) collective-permute-start(bf16[8,128,384]{2,1,0:T(8,128)(2,1)S(1)} %all_to_all.10.refs_0_), channel_id=1, source_target_pairs={{0,12},{192,228},{384,396},{576,612},{48,60},{240,276},{432,444},{... | collective-permute-start | bytes 2359304 | tf_op jit(solution)/shard_map/ppermute | solution.py:28
  47.9 1.9 %collective-permute-start.8 = (bf16[8,128,384]{2,1,0:T(8,128)(2,1)S(1)}, bf16[8,128,384]{2,1,0:T(8,128)(2,1)S(1)}, u32[]{:S(2)}, u32[]{:S(2)}) collective-permute-start(bf16[8,128,384]{2,1,0:T(8,128)(2,1)S(1)} %all_to_all.10.refs_0_), channel_id=1, source_target_pairs={{0,384},{192,720},{384,0},{576,240},{48,432},{240,576},{432,48},{6... | collective-permute-start | bytes 2359304 | tf_op jit(solution)/shard_map/ppermute | solution.py:28
  49.8 7.0 %collective-permute-start.3 = (bf16[8,128,384]{2,1,0:T(8,128)(2,1)S(1)}, bf16[8,128,384]{2,1,0:T(8,128)(2,1)S(1)}, u32[]{:S(2)}, u32[]{:S(2)}) collective-permute-start(bf16[8,128,384]{2,1,0:T(8,128)(2,1)S(1)} %all_to_all.10.refs_0_), channel_id=1, source_target_pairs={{0,396},{192,756},{384,12},{576,276},{48,444},{240,612},{432,60},{... | collective-permute-start | bytes 2359304 | tf_op jit(solution)/shard_map/ppermute | solution.py:28
  56.7 1.9 %collective-permute-start.5 = (bf16[8,128,384]{2,1,0:T(8,128)(2,1)S(1)}, bf16[8,128,384]{2,1,0:T(8,128)(2,1)S(1)}, u32[]{:S(2)}, u32[]{:S(2)}) collective-permute-start(bf16[8,128,384]{2,1,0:T(8,128)(2,1)S(1)} %all_to_all.10.refs_0_), channel_id=1, source_target_pairs={{0,192},{192,0},{384,576},{576,384},{48,240},{240,48},{432,624},{6... | collective-permute-start | bytes 2359304 | tf_op jit(solution)/shard_map/ppermute | solution.py:28
  58.7 1.2 %collective-permute-done.6.refs_2_ = bf16[8,128,384]{2,1,0:T(8,128)(2,1)S(1)} collective-permute-done((bf16[8,128,384]{2,1,0:T(8,128)(2,1)S(1)}, bf16[8,128,384]{2,1,0:T(8,128)(2,1)S(1)}, u32[]{:S(2)}, u32[]{:S(2)}) %collective-permute-start.6) | collective-permute-done | bytes 786464 | tf_op jit(solution)/shard_map/ppermute | solution.py:28
  59.9 3.3 %collective-permute-start.7 = (bf16[8,128,384]{2,1,0:T(8,128)(2,1)S(1)}, bf16[8,128,384]{2,1,0:T(8,128)(2,1)S(1)}, u32[]{:S(2)}, u32[]{:S(2)}) collective-permute-start(bf16[8,128,384]{2,1,0:T(8,128)(2,1)S(1)} %collective-permute-done.6.refs_2_), channel_id=1, source_target_pairs={{0,192},{192,0},{384,576},{576,384},{48,240},{240,48},{432,624},{6... | collective-permute-start | bytes 2359304 | tf_op jit(solution)/shard_map/ppermute | solution.py:28
  63.2 1.9 %collective-permute-start.9 = (bf16[8,128,384]{2,1,0:T(8,128)(2,1)S(1)}, bf16[8,128,384]{2,1,0:T(8,128)(2,1)S(1)}, u32[]{:S(2)}, u32[]{:S(2)}) collective-permute-start(bf16[8,128,384]{2,1,0:T(8,128)(2,1)S(1)} %collective-permute-done.8.refs_4_), channel_id=1, source_target_pairs={{0,192},{192,0},{384,576},{576,384},{48,240},{240,48},{432,624},{6... | collective-permute-start | bytes 2359304 | tf_op jit(solution)/shard_map/ppermute | solution.py:28
  65.2 7.5 %collective-permute-done.3.refs_0_ = bf16[8,128,384]{2,1,0:T(8,128)(2,1)S(1)} collective-permute-done((bf16[8,128,384]{2,1,0:T(8,128)(2,1)S(1)}, bf16[8,128,384]{2,1,0:T(8,128)(2,1)S(1)}, u32[]{:S(2)}, u32[]{:S(2)}) %collective-permute-start.3) | collective-permute-done | bytes 786464 | tf_op jit(solution)/shard_map/ppermute | solution.py:28
  72.6 2.4 %collective-permute-start.4 = (bf16[8,128,384]{2,1,0:T(8,128)(2,1)S(1)}, bf16[8,128,384]{2,1,0:T(8,128)(2,1)S(1)}, u32[]{:S(2)}, u32[]{:S(2)}) collective-permute-start(bf16[8,128,384]{2,1,0:T(8,128)(2,1)S(1)} %collective-permute-done.3.refs_0_), channel_id=1, source_target_pairs={{0,192},{192,0},{384,576},{576,384},{48,240},{240,48},{432,624},{6... | collective-permute-start | bytes 2359304 | tf_op jit(solution)/shard_map/ppermute | solution.py:28
  75.0 2.7 %collective-permute-start = (f32[128,384]{1,0:T(8,128)S(1)}, f32[128,384]{1,0:T(8,128)S(1)}, u32[]{:S(2)}, u32[]{:S(2)}) collective-permute-start(f32[128,384]{1,0:T(8,128)S(1)} %get-tuple-element.7.own_ref), channel_id=1, source_target_pairs={{0,384},{192,576},{384,0},{576,192},{48,432},{240,624},{432,48},{6... | collective-permute-start | bytes 589832 | tf_op jit(solution)/shard_map/ppermute | solution.py:28
  77.7 5.7 %collective-permute-done.y_ref = f32[128,384]{1,0:T(8,128)S(1)} collective-permute-done((f32[128,384]{1,0:T(8,128)S(1)}, f32[128,384]{1,0:T(8,128)S(1)}, u32[]{:S(2)}, u32[]{:S(2)}) %collective-permute-start) | collective-permute-done | bytes 196640 | tf_op jit(solution)/shard_map/ppermute | solution.py:28
  83.4 2.8 %collective-permute-start.1 = (f32[128,384]{1,0:T(8,128)S(1)}, f32[128,384]{1,0:T(8,128)S(1)}, u32[]{:S(2)}, u32[]{:S(2)}) collective-permute-start(f32[128,384]{1,0:T(8,128)S(1)} %get-tuple-element.7.own_ref), channel_id=1, source_target_pairs={{0,192},{192,0},{384,576},{576,384},{48,240},{240,48},{432,624},{6... | collective-permute-start | bytes 589832 | tf_op jit(solution)/shard_map/ppermute | solution.py:28
  86.1 1.0 %collective-permute-done.1.core_ref = f32[128,384]{1,0:T(8,128)S(1)} collective-permute-done((f32[128,384]{1,0:T(8,128)S(1)}, f32[128,384]{1,0:T(8,128)S(1)}, u32[]{:S(2)}, u32[]{:S(2)}) %collective-permute-start.1) | collective-permute-done | bytes 196640 | tf_op jit(solution)/shard_map/ppermute | solution.py:28
  87.2 2.3 %collective-permute-start.2 = (f32[128,384]{1,0:T(8,128)S(1)}, f32[128,384]{1,0:T(8,128)S(1)}, u32[]{:S(2)}, u32[]{:S(2)}) collective-permute-start(f32[128,384]{1,0:T(8,128)S(1)} %collective-permute-done.y_ref), channel_id=1, source_target_pairs={{0,192},{192,0},{384,576},{576,384},{48,240},{240,48},{432,624},{6... | collective-permute-start | bytes 589832 | tf_op jit(solution)/shard_map/ppermute | solution.py:28
  89.5 1.0 %collective-permute-done.2.both_ref = f32[128,384]{1,0:T(8,128)S(1)} collective-permute-done((f32[128,384]{1,0:T(8,128)S(1)}, f32[128,384]{1,0:T(8,128)S(1)}, u32[]{:S(2)}, u32[]{:S(2)}) %collective-permute-start.2) | collective-permute-done | bytes 196640 | tf_op jit(solution)/shard_map/ppermute | solution.py:28
  90.5 1.1 %copy-done = f32[512,384]{1,0:T(8,128)S(1)} copy-done((f32[512,384]{1,0:T(8,128)S(1)}, f32[512,384]{1,0:T(8,128)}, u32[]{:S(2)}) %copy-start) | copy-done | bytes 786456
  91.6 1.1 %copy-done.1 = f32[512,384]{1,0:T(8,128)S(1)} copy-done((f32[512,384]{1,0:T(8,128)S(1)}, f32[512,384]{1,0:T(8,128)}, u32[]{:S(2)}) %copy-start.1) | copy-done | bytes 786456
  92.8 1.3 %whole.1 = (f32[512,384]{1,0:T(8,128)}, f32[512,384]{1,0:T(8,128)}) custom-call(f32[128,384]{1,0:T(8,128)S(1)} %get-tuple-element.7.own_ref, f32[128,384]{1,0:T(8,128)S(1)} %collective-permute-done.y_ref, f32[128,384]{1,0:T(8,128)S(1)} %collective-permute-done.1.core_ref, f32[128,384]{1,0:T(8,128)S(1)} %collective-permute-done.2.both_ref, ...), custom_call_target="tpu_custom_call" | custom-call | flops 1000000 | bytes 5242880 | tf_op jit(solution)/shard_map/whole/pallas_call | solution.py:161
  94.1 2.6 %place.3.refs_1_ = bf16[8192,384]{1,0:T(8,128)(2,1)} custom-call(bf16[8,128,384]{2,1,0:T(8,128)(2,1)S(1)} %all_to_all.10.refs_0_, bf16[8,128,384]{2,1,0:T(8,128)(2,1)S(1)} %collective-permute-done.5.refs_1_, bf16[8,128,384]{2,1,0:T(8,128)(2,1)S(1)} %collective-permute-done.6.refs_2_, bf16[8,128,384]{2,1,0:T(8,128)(2,1)S(1)} %collective-permute-done.7.refs_3_, ...), custom_call_target="tpu_custom_call" | custom-call | flops 6000000 | bytes 9437184 | tf_op jit(solution)/shard_map/place/pallas_call | solution.py:91
  96.7 1.0 place.4.refs_1_
  (9 shorter events, 1.1 us)
Async XLA Ops:
  0.6 20.4 %all-to-all-start = ((bf16[4,128,384]{2,1,0:T(8,128)(2,1)}), bf16[4,128,384]{2,1,0:T(8,128)(2,1)S(1)}, u32[]{:S(2)}, u32[]{:S(2)}) async-start(bf16[4,128,384]{2,1,0:T(8,128)(2,1)} %bitcast.1), calls=%async_computation | async-start | bytes 786432 | tf_op jit(solution)/shard_map/all_to_all | solution.py:117
  45.9 13.9 %collective-permute-start.6 = (bf16[8,128,384]{2,1,0:T(8,128)(2,1)S(1)}, bf16[8,128,384]{2,1,0:T(8,128)(2,1)S(1)}, u32[]{:S(2)}, u32[]{:S(2)}) collective-permute-start(bf16[8,128,384]{2,1,0:T(8,128)(2,1)S(1)} %all_to_all.10.refs_0_), channel_id=1, source_target_pairs={{0,12},{192,228},{384,396},{576,612},{48,60},{240,276},{432,444},{... | collective-permute-start | bytes 2359304 | tf_op jit(solution)/shard_map/ppermute | solution.py:28
  47.9 15.4 %collective-permute-start.8 = (bf16[8,128,384]{2,1,0:T(8,128)(2,1)S(1)}, bf16[8,128,384]{2,1,0:T(8,128)(2,1)S(1)}, u32[]{:S(2)}, u32[]{:S(2)}) collective-permute-start(bf16[8,128,384]{2,1,0:T(8,128)(2,1)S(1)} %all_to_all.10.refs_0_), channel_id=1, source_target_pairs={{0,384},{192,720},{384,0},{576,240},{48,432},{240,576},{432,48},{6... | collective-permute-start | bytes 2359304 | tf_op jit(solution)/shard_map/ppermute | solution.py:28
  49.8 22.8 %collective-permute-start.3 = (bf16[8,128,384]{2,1,0:T(8,128)(2,1)S(1)}, bf16[8,128,384]{2,1,0:T(8,128)(2,1)S(1)}, u32[]{:S(2)}, u32[]{:S(2)}) collective-permute-start(bf16[8,128,384]{2,1,0:T(8,128)(2,1)S(1)} %all_to_all.10.refs_0_), channel_id=1, source_target_pairs={{0,396},{192,756},{384,12},{576,276},{48,444},{240,612},{432,60},{... | collective-permute-start | bytes 2359304 | tf_op jit(solution)/shard_map/ppermute | solution.py:28
  56.7 37.4 %collective-permute-start.5 = (bf16[8,128,384]{2,1,0:T(8,128)(2,1)S(1)}, bf16[8,128,384]{2,1,0:T(8,128)(2,1)S(1)}, u32[]{:S(2)}, u32[]{:S(2)}) collective-permute-start(bf16[8,128,384]{2,1,0:T(8,128)(2,1)S(1)} %all_to_all.10.refs_0_), channel_id=1, source_target_pairs={{0,192},{192,0},{384,576},{576,384},{48,240},{240,48},{432,624},{6... | collective-permute-start | bytes 2359304 | tf_op jit(solution)/shard_map/ppermute | solution.py:28
  59.9 34.2 %collective-permute-start.7 = (bf16[8,128,384]{2,1,0:T(8,128)(2,1)S(1)}, bf16[8,128,384]{2,1,0:T(8,128)(2,1)S(1)}, u32[]{:S(2)}, u32[]{:S(2)}) collective-permute-start(bf16[8,128,384]{2,1,0:T(8,128)(2,1)S(1)} %collective-permute-done.6.refs_2_), channel_id=1, source_target_pairs={{0,192},{192,0},{384,576},{576,384},{48,240},{240,48},{432,624},{6... | collective-permute-start | bytes 2359304 | tf_op jit(solution)/shard_map/ppermute | solution.py:28
  63.2 30.9 %collective-permute-start.9 = (bf16[8,128,384]{2,1,0:T(8,128)(2,1)S(1)}, bf16[8,128,384]{2,1,0:T(8,128)(2,1)S(1)}, u32[]{:S(2)}, u32[]{:S(2)}) collective-permute-start(bf16[8,128,384]{2,1,0:T(8,128)(2,1)S(1)} %collective-permute-done.8.refs_4_), channel_id=1, source_target_pairs={{0,192},{192,0},{384,576},{576,384},{48,240},{240,48},{432,624},{6... | collective-permute-start | bytes 2359304 | tf_op jit(solution)/shard_map/ppermute | solution.py:28
  72.6 25.1 %collective-permute-start.4 = (bf16[8,128,384]{2,1,0:T(8,128)(2,1)S(1)}, bf16[8,128,384]{2,1,0:T(8,128)(2,1)S(1)}, u32[]{:S(2)}, u32[]{:S(2)}) collective-permute-start(bf16[8,128,384]{2,1,0:T(8,128)(2,1)S(1)} %collective-permute-done.3.refs_0_), channel_id=1, source_target_pairs={{0,192},{192,0},{384,576},{576,384},{48,240},{240,48},{432,624},{6... | collective-permute-start | bytes 2359304 | tf_op jit(solution)/shard_map/ppermute | solution.py:28
  75.0 8.3 %collective-permute-start = (f32[128,384]{1,0:T(8,128)S(1)}, f32[128,384]{1,0:T(8,128)S(1)}, u32[]{:S(2)}, u32[]{:S(2)}) collective-permute-start(f32[128,384]{1,0:T(8,128)S(1)} %get-tuple-element.7.own_ref), channel_id=1, source_target_pairs={{0,384},{192,576},{384,0},{576,192},{48,432},{240,624},{432,48},{6... | collective-permute-start | bytes 589832 | tf_op jit(solution)/shard_map/ppermute | solution.py:28
  83.4 3.8 %collective-permute-start.1 = (f32[128,384]{1,0:T(8,128)S(1)}, f32[128,384]{1,0:T(8,128)S(1)}, u32[]{:S(2)}, u32[]{:S(2)}) collective-permute-start(f32[128,384]{1,0:T(8,128)S(1)} %get-tuple-element.7.own_ref), channel_id=1, source_target_pairs={{0,192},{192,0},{384,576},{576,384},{48,240},{240,48},{432,624},{6... | collective-permute-start | bytes 589832 | tf_op jit(solution)/shard_map/ppermute | solution.py:28
  87.2 3.3 %collective-permute-start.2 = (f32[128,384]{1,0:T(8,128)S(1)}, f32[128,384]{1,0:T(8,128)S(1)}, u32[]{:S(2)}, u32[]{:S(2)}) collective-permute-start(f32[128,384]{1,0:T(8,128)S(1)} %collective-permute-done.y_ref), channel_id=1, source_target_pairs={{0,192},{192,0},{384,576},{576,384},{48,240},{240,48},{432,624},{6... | collective-permute-start | bytes 589832 | tf_op jit(solution)/shard_map/ppermute | solution.py:28
  90.5 1.1 %copy-start = (f32[512,384]{1,0:T(8,128)S(1)}, f32[512,384]{1,0:T(8,128)}, u32[]{:S(2)}) copy-start(f32[512,384]{1,0:T(8,128)} %momentum_ref.1) | copy-start | bytes 2359300
  91.6 1.1 %copy-start.1 = (f32[512,384]{1,0:T(8,128)S(1)}, f32[512,384]{1,0:T(8,128)}, u32[]{:S(2)}) copy-start(f32[512,384]{1,0:T(8,128)} %params_ref.1) | copy-start | bytes 2359300
